TPU v7x, 256 devices: a whole 4x4x8 slice. The times are simulated.
256 devices in a mesh: dp: 64 (over z_lo, x, y, core), vocab: 4 (over z_hi).
Axes of the slice: x: 4, y: 4, z: 8 (z_hi: 4, z_lo: 2; z = z_hi * 2 + z_lo), core: 2. Of those that a mesh axis runs over, the one named last changes fastest.
Arguments:
- hidden: bfloat16 [512, 4096], P('dp'), may hold values from -16 to 16
- embed_grad: bfloat16 [512, 4096], P('dp'), may hold values from -8 to 8
- token_ids: int32 [512], P('dp'), may hold values from 0 to 32767
- loss_weight: float32 [512], P('dp'), may hold values from 16 to 256
- teacher_logits: bfloat16 [512, 32768], P('dp', 'vocab'), may hold values from -24 to 256
- head: bfloat16 [4096, 32768], P('dp', 'vocab'), may hold values from -1 to 1
Outputs:
- grad_hidden: bfloat16 [512, 4096], P('dp', 'vocab')
- head_grad: float32 [4096, 32768], P('dp', 'vocab')
Inputs may be any that keep to these rules, and one draw needn't show every extreme that they name: `token_ids`: token ids of the vocabulary window.
All inputs are finite; a program needn't handle non-finite values.
Results may differ from a plain program's by a relative error of at most 0.0022.
The roundings to bfloat16 on the way count: a program that leaves them out, or rounds other values in their place, can miss the bound.
Values may be sent and summed in bfloat16 or wider, within the bound.
No kernel may reach another device: no remote copies, remote signals or barrier semaphores. Data moves between devices by JAX's collectives and lax.ppermute only.
A program may use at most 128 MiB of HBM per device.

v0:
```python
import jax
import jax.numpy as jnp
from jax import lax
from jax.sharding import Mesh
from jax.sharding import PartitionSpec as P

DP = ("dp_0", "dp_1", "dp_2", "dp_3")


def split_up(x, dim, devices):
    lengths = x.shape
    parts = x.reshape(*lengths[:dim], devices, lengths[dim] // devices, *lengths[dim + 1 :])
    return jnp.moveaxis(parts, dim, 0)


def sum_by_chip(x, chips, core, dim):
    sizes = (lax.axis_size(chips), lax.axis_size(core))
    parts = split_up(x, dim, sizes[0] * sizes[1])
    inside = parts.shape[1:]
    parts = parts.reshape(*sizes, *inside).swapaxes(0, 1).reshape(-1, *inside)
    parts = lax.psum_scatter(parts, core, scatter_dimension=0, tiled=True)
    return lax.psum_scatter(parts, chips, scatter_dimension=0, tiled=True)[0]


def sent_to_all(x, axis):
    devices = lax.axis_size(axis)
    return lax.all_to_all(jnp.broadcast_to(x[None], (devices, *x.shape)), axis, 0, 0, tiled=True)


def all_in_one(x, axis):
    leaves = jax.tree.leaves(x)
    turns = sorted(range(len(leaves)), key=lambda k: -leaves[k].size)
    width = (1, *leaves[turns[0]].shape)[-1]
    lines = [
        jnp.pad(leaves[k].reshape(-1), (0, -leaves[k].size % width)).reshape(-1, width)
        for k in turns
    ]
    both, at, found = (sent_to_all(jnp.concatenate(lines), axis), 0, {})
    for k, line in zip(turns, lines):
        piece = both[:, at : at + len(line)].reshape(len(both), -1)
        found[k] = piece[:, : leaves[k].size].reshape(-1, *leaves[k].shape)
        at += len(line)
    numbers = iter(range(len(leaves)))
    return jax.tree.map(lambda _: found[next(numbers)], x)


def folded_in_pairs(pieces, combine):
    while len(jax.tree.leaves(pieces)[0]) > 1:
        pieces = jax.vmap(combine)(
            *(jax.tree.map(lambda part: part[side::2], pieces) for side in (0, 1))
        )
    return jax.tree.map(lambda part: part[0], pieces)


def merged(x, axis, combine):
    pieces = all_in_one(x, axis)
    return folded_in_pairs(pieces, combine)


def summed_on_arrival(x, axis, dim):
    parts = split_up(x, dim, lax.axis_size(axis))
    arrived = lax.all_to_all(parts, axis, split_axis=0, concat_axis=0, tiled=True)
    return arrived.sum(axis=0)


def contract_rows(left, right):
    return lax.dot_general(
        left, right, (((0,), (0,)), ((), ())), preferred_element_type=jnp.float32
    )


def contract_cols(left, right):
    return lax.dot_general(
        left, right, (((1,), (1,)), ((), ())), preferred_element_type=jnp.float32
    )


def combine_pairs(earlier, later):
    s_max_a, s_sum_a, t_max_a, t_sum_a = earlier
    s_max_b, s_sum_b, t_max_b, t_sum_b = later
    s_max = jnp.maximum(s_max_a, s_max_b)
    t_max = jnp.maximum(t_max_a, t_max_b)
    s_sum = s_sum_a * jnp.exp(s_max_a - s_max) + s_sum_b * jnp.exp(s_max_b - s_max)
    t_sum = t_sum_a * jnp.exp(t_max_a - t_max) + t_sum_b * jnp.exp(t_max_b - t_max)
    return (s_max, s_sum, t_max, t_sum)


def per_device(hidden, embed_grad, token_ids, loss_weight, teacher_logits, head):
    vocab_width = head.shape[1]
    hidden_cols, embed_cols = (
        lax.all_to_all(hidden, DP, split_axis=1, concat_axis=0, tiled=True),
        lax.all_to_all(embed_grad, DP, split_axis=1, concat_axis=0, tiled=True),
    )
    student = sum_by_chip(
        jnp.dot(hidden_cols, head, preferred_element_type=jnp.float32),
        ("dp_0", "dp_1", "dp_2"),
        "dp_3",
        0,
    )
    teacher = teacher_logits.astype(jnp.float32)
    student_max = jnp.max(student, axis=1)
    teacher_max = jnp.max(teacher, axis=1)
    student_sum = jnp.sum(jnp.exp(student - student_max[:, None]), axis=1)
    teacher_sum = jnp.sum(jnp.exp(teacher - teacher_max[:, None]), axis=1)
    student_top, student_total, teacher_top, teacher_total = merged(
        (student_max, student_sum, teacher_max, teacher_sum), "vocab", combine_pairs
    )
    student_norm = student_top + jnp.log(student_total)
    teacher_norm = teacher_top + jnp.log(teacher_total)
    gap = (
        loss_weight[:, None]
        * (jnp.exp(student - student_norm[:, None]) - jnp.exp(teacher - teacher_norm[:, None]))
    ).astype(jnp.bfloat16)
    vocab_ids = lax.axis_index("vocab") * vocab_width + jnp.arange(vocab_width, dtype=jnp.int32)
    gap_piece = lax.all_gather(gap, DP, axis=0, tiled=True)
    id_piece = lax.all_gather(token_ids, DP, axis=0, tiled=True)
    lookup = (id_piece[:, None] == vocab_ids[None, :]).astype(jnp.bfloat16)
    grad_rows = contract_rows(hidden_cols, gap_piece) + contract_rows(embed_cols, lookup)
    back_cols = contract_cols(gap_piece, head)
    head_grad, back_cols = (grad_rows, back_cols)
    regrouped = lax.all_to_all(back_cols, DP, split_axis=0, concat_axis=1, tiled=True)
    grad_hidden = summed_on_arrival(regrouped, "vocab", 1).astype(jnp.bfloat16)
    return (grad_hidden, head_grad)


def solution(mesh):
    torus = Mesh(
        mesh.devices.reshape(2, 4, 4, 2, mesh.shape["vocab"]),
        ("dp_0", "dp_1", "dp_2", "dp_3", "vocab"),
    )
    in_specs = (P(DP, None), P(DP, None), P(DP), P(DP), P(DP, "vocab"), P(DP, "vocab"))
    out_specs = (P(DP, "vocab"), P(DP, "vocab"))
    return jax.shard_map(
        per_device, mesh=torus, in_specs=in_specs, out_specs=out_specs, check_vma=False
    )
```

profile of v0, /device:TPU:2, one launch (start us, length us, event | category | flops | bytes accessed | tf_op | source)
XLA Modules:
  0.0 424.2 jit_solution(6314430800878000126)
XLA Ops:
  7.2 1.1 all_to_all.46
  8.6 16.4 %all_to_all.64 = bf16[64,2,256]{2,1,0:T(2,128)(2,1)S(1)} all-to-all(bf16[64,2,256]{2,1,0:T(2,128)(2,1)S(1)} %reshape.104), channel_id=1, replica_groups=mesh['dp_0'=2,'dp_1'=4,'dp_2'=4,'dp_3'=2,'vocab'=4] {'dp_0','dp_1','dp_2..., dimensions={0} | all-to-all | bytes 131072 | tf_op jit(solution)/shard_map/all_to_all | solution.py:91
  25.1 2.3 convolution_bitcast_fusion
  27.4 6.1 %copy.15 = f32[2,32,8,8192]{3,2,1,0:T(8,128)} copy(f32[2,32,8,8192]{3,2,0,1:T(8,128)S(1)} %convolution_bitcast_fusion) | data formatting | bytes 33554432 | tf_op jit(solution)/shard_map/transpose | solution.py:20
  33.7 29.8 %reduce-scatter.3.cloned.1.call-done = f32[32,8,8192]{2,1,0:T(8,128)} async-done(((f32[64,8,8192]{2,1,0:T(8,128)}), f32[32,8,8192]{2,1,0:T(8,128)}) %reduce-scatter.3.cloned.1.call-update) | async-done | bytes 8388624 | tf_op jit(solution)/shard_map/reduce_scatter | solution.py:21
  64.0 179.9 %reduce-scatter.5.cloned.1.call-done = f32[1,8,8192]{2,1,0:T(8,128)} async-done(((f32[32,8,8192]{2,1,0:T(8,128)}), f32[1,8,8192]{2,1,0:T(8,128)}) %reduce-scatter.5.cloned.1.call-update) | async-done | bytes 262160 | tf_op jit(solution)/shard_map/reduce_scatter | solution.py:22
  243.9 1.1 reduce_max.27
  245.1 1.2 fusion.13
  246.3 14.1 %all_to_all.65 = f32[4,4,8]{2,1,0:T(4,128)S(1)} all-to-all(f32[4,4,8]{2,1,0:T(4,128)S(1)} %broadcast_in_dim.2), channel_id=1, replica_groups=mesh['dp_0'=2,'dp_1'=4,'dp_2'=4,'dp_3'=2,'vocab'=4] {'vocab'}, dimensions={0} | all-to-all | bytes 1024 | tf_op jit(solution)/shard_map/all_to_all | solution.py:27
  260.6 1.8 fusion.11
  263.5 12.4 %all-to-all-start.4 = ((bf16[64,2,256]{2,1,0:T(2,128)(2,1)}), bf16[64,2,256]{2,1,0:T(2,128)(2,1)S(1)}, u32[]{:S(2)}, u32[]{:S(2)}) async-start(bf16[64,2,256]{2,1,0:T(2,128)(2,1)} %reshape.108), calls=%async_computation.6 | async-start | bytes 131072 | tf_op jit(solution)/shard_map/all_to_all | solution.py:92
  277.4 18.7 %all-reduce = s32[512]{0:T(512)S(1)} all-reduce(s32[512]{0:T(512)S(1)} %dynamic-update-slice), channel_id=1, replica_groups=mesh['dp_0'=2,'dp_1'=4,'dp_2'=4,'dp_3'=2,'vocab'=4] {'dp_0','dp_1','dp_2..., use_global_device_ids=true, to_apply=%add | all-reduce | flops 512 | bytes 4096
  296.9 77.7 %all-gather.2.cloned.1.call-done = bf16[512,8192]{1,0:T(8,128)(2,1)} async-done(((bf16[8,8192]{1,0:T(8,128)(2,1)}), bf16[512,8192]{1,0:T(8,128)(2,1)}) %all-gather.2.cloned.1.call-update) | async-done | bytes 8388624 | tf_op jit(solution)/shard_map/all_gather | solution.py:115
  374.6 5.7 %convolution_bitcast_fusion.1 = f32[64,8,64]{2,1,0:T(8,128)S(1)} fusion(bf16[512,8192]{1,0:T(8,128)(2,1)} %all-gather.2.cloned.1.call-done, bf16[64,8192]{1,0:T(8,128)(2,1)S(1)} %copy-done), kind=kOutput, calls=%fused_computation.7 | convolution fusion | flops 536870912 | bytes 9568256 | tf_op jit(solution)/shard_map/dot_general | solution.py:73
  380.3 0.8 reshape.106
  381.2 6.9 %all-to-all-start.2 = ((f32[64,1,512]{2,1,0:T(1,128)}), f32[64,1,512]{2,1,0:T(1,128)S(1)}, u32[]{:S(2)}, u32[]{:S(2)}) async-start(f32[64,1,512]{2,1,0:T(1,128)} %reshape.106), calls=%async_computation.4 | async-start | bytes 262144 | tf_op jit(solution)/shard_map/all_to_all | solution.py:121
  388.1 3.8 fusion
  391.8 3.7 all-to-all-done.2
  396.1 1.6 reduce.2
  397.7 1.0 reshape.107
  399.4 1.1 reshape.96
  401.3 6.5 %all-to-all-start.3 = ((f32[4,8,1024]{2,1,0:T(8,128)}), f32[4,8,1024]{2,1,0:T(8,128)S(1)}, u32[]{:S(2)}, u32[]{:S(2)}) async-start(f32[4,8,1024]{2,1,0:T(8,128)} %copy.18), calls=%async_computation.5 | async-start | bytes 262144 | tf_op jit(solution)/shard_map/all_to_all | solution.py:62
  407.8 6.3 %fusion.2 = f32[64,8192]{1,0:T(8,128)} fusion(f32[8192,64]{0,1:T(8,128)S(1)} %fusion, bf16[512,8192]{1,0:T(8,128)(2,1)} %all-gather.2.cloned.1.call-done, bf16[64,8,64]{2,1,0:T(8,128)(2,1)S(1)} %reshape.105), kind=kOutput, calls=%fused_computation.4 | convolution fusion | flops 537395200 | bytes 12648448 | tf_op jit(solution)/shard_map/dot_general | solution.py:67
  414.1 2.9 all-to-all-done.3
  (51 shorter events, 6.6 us)
Async XLA Ops:
  7.2 17.9 %copy-start = (bf16[64,8192]{1,0:T(8,128)(2,1)S(1)}, bf16[64,8192]{1,0:T(8,128)(2,1)}, u32[]{:S(2)}) copy-start(bf16[64,8192]{1,0:T(8,128)(2,1)} %param.11) | copy-start | bytes 3145732
  7.2 56.3 %reduce-scatter.3.cloned.1.call-start = ((), (), s32[]{:S(2)}) async-start(), calls=%async_computation.7 | async-start | bytes 25165824 | tf_op jit(solution)/shard_map/reduce_scatter | solution.py:21
  33.6 30.0 %copy-start.1 = (bf16[8,8192]{1,0:T(8,128)(2,1)S(1)}, bf16[8,8192]{1,0:T(8,128)(2,1)}, u32[]{:S(2)}) copy-start(bf16[8,8192]{1,0:T(8,128)(2,1)} %param.10) | copy-start | bytes 393220
  33.6 227.0 %copy-start.3 = (f32[8]{0:T(128)S(1)}, f32[8]{0:T(128)}, u32[]{:S(2)}) copy-start(f32[8]{0:T(128)} %param.9) | copy-start | bytes 100
  33.6 228.8 %copy-start.2 = (bf16[8,4096]{1,0:T(8,128)(2,1)S(1)}, bf16[8,4096]{1,0:T(8,128)(2,1)}, u32[]{:S(2)}) copy-start(bf16[8,4096]{1,0:T(8,128)(2,1)} %param.7) | copy-start | bytes 196612
  33.6 242.3 %copy-start.5 = (u32[256]{0:T(256)S(1)}, u32[256]{0:T(256)}, u32[]{:S(2)}) copy-start(u32[256]{0:T(256)} %constant.20) | copy-start | bytes 3076
  33.6 243.5 %copy-start.4 = (s32[8]{0:T(128)S(1)}, s32[8]{0:T(128)}, u32[]{:S(2)}) copy-start(s32[8]{0:T(128)} %param.8) | copy-start | bytes 100
  33.6 210.3 %reduce-scatter.5.cloned.1.call-start = ((), (), s32[]{:S(2)}) async-start(), calls=%async_computation.8 | async-start | bytes 8650752 | tf_op jit(solution)/shard_map/reduce_scatter | solution.py:22
  63.5 311.1 %all-gather.2.cloned.1.call-start = ((), (), s32[]{:S(2)}) async-start(), calls=%async_computation.9 | async-start | bytes 8519680 | tf_op jit(solution)/shard_map/all_gather | solution.py:115
  263.5 33.3 %all-to-all-start.4 = ((bf16[64,2,256]{2,1,0:T(2,128)(2,1)}), bf16[64,2,256]{2,1,0:T(2,128)(2,1)S(1)}, u32[]{:S(2)}, u32[]{:S(2)}) async-start(bf16[64,2,256]{2,1,0:T(2,128)(2,1)} %reshape.108), calls=%async_computation.6 | async-start | bytes 131072 | tf_op jit(solution)/shard_map/all_to_all | solution.py:92
  381.2 14.4 %all-to-all-start.2 = ((f32[64,1,512]{2,1,0:T(1,128)}), f32[64,1,512]{2,1,0:T(1,128)S(1)}, u32[]{:S(2)}, u32[]{:S(2)}) async-start(f32[64,1,512]{2,1,0:T(1,128)} %reshape.106), calls=%async_computation.4 | async-start | bytes 262144 | tf_op jit(solution)/shard_map/all_to_all | solution.py:121
  401.3 15.8 %all-to-all-start.3 = ((f32[4,8,1024]{2,1,0:T(8,128)}), f32[4,8,1024]{2,1,0:T(8,128)S(1)}, u32[]{:S(2)}, u32[]{:S(2)}) async-start(f32[4,8,1024]{2,1,0:T(8,128)} %copy.18), calls=%async_computation.5 | async-start | bytes 262144 | tf_op jit(solution)/shard_map/all_to_all | solution.py:62
Sparse Core Ops, SparseCore 0:
  33.7 29.7 reduce-scatter.2
  66.1 177.8 reduce-scatter.4
  262.5 112.0 all-gather.1
where the time goes:
time: 425 us; the launch traced here: 424 us
  waiting for transfers between devices  294 us (69%)
  blocking collectives  49.2 us (12%)
  starting transfers between devices  25.9 us (6%)
  matrix products  18.1 us (4%)
  local copies, waits for them, and re-layouts  14.8 us (3%)
  between operations  14.6 us (3%)
  other arithmetic  7.42 us (2%)
    reduce_scatter x1, waiting for transfers between devices, sum_by_chip(): return lax.psum_scatter(parts, chips, scatter_dimension=0, tiled=True)[0]  180 us
    all_gather x1, waiting for transfers between devices, per_device(): gap_piece = lax.all_gather(gap, DP, axis=0, tiled=True)  77.7 us
    reduce_scatter x1, waiting for transfers between devices, sum_by_chip(): parts = lax.psum_scatter(parts, core, scatter_dimension=0, tiled=True)  29.8 us
    unnamed x1, blocking collectives  18.7 us
    all_to_all x1, blocking collectives, per_device(): lax.all_to_all(hidden, DP, split_axis=1, concat_axis=0, tiled=True)  16.4 us
    all_to_all x1, blocking collectives, sent_to_all(): lax.all_to_all(jnp.broadcast_to(x[None], (devices, *x.shape)), axis, 0, 0...  14.1 us
    all_to_all x1, starting transfers between devices, per_device(): lax.all_to_all(embed_grad, DP, split_axis=1, concat_axis=0, tiled=True)  12.4 us
    dot_general x2, matrix products, contract_rows(): lax.dot_general(left, right, (((0,), (0,)), ((), ())), preferred_element_...  10.1 us
  transfers between devices with their start and end apart: 6, of which 5 were waited for; matrix products, arithmetic and copies ran while one was open for 3% of the time, Pallas kernels for 0%

commit v1 on v0

v1 whole, which is shorter than its diff:
```python
import jax
import jax.numpy as jnp
from jax import lax
from jax.sharding import Mesh
from jax.sharding import PartitionSpec as P

DP = ("z", "x", "y", "c")
COLS = ("z", "x", "c")


def exchange(x, axes):
    return lax.all_to_all(x, axes, 0, 0, tiled=True)


def in_pieces(x, count):
    pieces = []
    for _ in range(count):
        piece = lax.reduce_precision(x, 8, 7)
        pieces.append(piece.astype(jnp.bfloat16))
        x = x - piece
    return jnp.stack(pieces, axis=-1)


def dot(left, right, contract):
    return lax.dot_general(left, right, (contract, ((), ())), preferred_element_type=jnp.float32)


def per_device(hidden, embed_grad, token_ids, loss_weight, teacher_logits, head):
    bf16, f32 = jnp.bfloat16, jnp.float32
    sizes = {axis: lax.axis_size(axis) for axis in DP + ("vocab",)}
    nz, nx, ny, nc, nv = (sizes[axis] for axis in DP + ("vocab",))
    own, width = hidden.shape
    rows, vocab = head.shape
    cols = nz * nx * nc
    devices = cols * ny
    block = vocab // cols
    tokens = devices * own
    part = cols * rows

    hidden_out = hidden.reshape(own, nz * nx, ny, nc * rows)
    hidden_out = hidden_out.transpose(2, 0, 1, 3).reshape(ny, 1, own, part)
    hidden_out = jnp.broadcast_to(hidden_out, (ny, cols, own, part)).reshape(devices, own, part)
    embed_out = embed_grad.reshape(own, nz * nx, ny, nc, rows)
    embed_out = embed_out.transpose(2, 1, 3, 0, 4).reshape(devices, own, rows)
    id_high = token_ids // 256
    extra = jnp.concatenate(
        [
            id_high[:, None].astype(bf16),
            (token_ids - 256 * id_high)[:, None].astype(bf16),
            in_pieces(loss_weight, 3),
        ],
        axis=1,
    )
    extra = jnp.pad(extra, ((0, 0), (0, 128 - rows - extra.shape[1])))
    extra = jnp.broadcast_to(extra[None], (devices, *extra.shape))
    sent = jnp.concatenate([hidden_out, embed_out, extra], axis=2)
    mine = exchange(sent, ("y", "z", "x", "c")).reshape(tokens, part + 128)
    hidden_part = mine[:, :part]
    embed_cols = mine[:, part : part + rows]
    ids = mine[:, part + rows : part + rows + 2].astype(jnp.int32)
    ids = ids[:, 0] * 256 + ids[:, 1]
    weights = mine[:, part + rows + 2 : part + rows + 5].astype(f32)
    weights = weights[:, 0] + weights[:, 1] + weights[:, 2]
    weights = lax.dynamic_index_in_dim(
        weights.reshape(ny, cols * own), lax.axis_index("y"), 0, keepdims=False
    )

    stacked = jnp.concatenate([head, teacher_logits], axis=0).reshape(rows + own, cols, block)
    stacked = exchange(stacked.swapaxes(0, 1), COLS)
    head_part = stacked[:, :rows].reshape(part, block)
    teacher = stacked[:, rows:].reshape(cols * own, block).astype(f32)

    student = dot(hidden_part, head_part, ((1,), (0,))).reshape(ny, cols * own, block)
    student = exchange(student, "y").sum(axis=0)

    student_max = jnp.max(student, axis=1)
    teacher_max = jnp.max(teacher, axis=1)
    student_sum = jnp.sum(jnp.exp(student - student_max[:, None]), axis=1)
    teacher_sum = jnp.sum(jnp.exp(teacher - teacher_max[:, None]), axis=1)
    stats = jnp.stack([student_max, teacher_max, student_sum, teacher_sum])
    stats = exchange(
        jnp.broadcast_to(stats[None], (cols * nv, *stats.shape)), COLS + ("vocab",)
    )
    tops = jnp.max(stats[:, :2], axis=0)
    totals = jnp.sum(stats[:, 2:] * jnp.exp(stats[:, :2] - tops), axis=0)
    norms = tops + jnp.log(totals)
    gap = (
        weights[:, None]
        * (jnp.exp(student - norms[0][:, None]) - jnp.exp(teacher - norms[1][:, None]))
    ).astype(bf16)
    gap = exchange(jnp.broadcast_to(gap[None], (ny, *gap.shape)), "y")

    gap_rows = gap.reshape(tokens, block)
    gap_by_core = gap.reshape(ny, nz * nx, nc, own, block).transpose(2, 1, 0, 3, 4)
    back = dot(gap_by_core.reshape(tokens, block), head_part, ((1,), (1,)))
    back = exchange(back.reshape(nc, tokens // nc, part), "c").sum(axis=0)
    back = exchange(back.reshape(nz * nx, ny * own, part), ("z", "x")).sum(axis=0)
    back = back.reshape(ny, own, nv, part // nv).transpose(0, 2, 1, 3)
    back = exchange(back.reshape(ny * nv, own, part // nv), ("y", "vocab"))
    back = back.reshape(ny, nv, own, part // nv).sum(axis=1)
    back = back.reshape(ny, own, part // nv // (nc * rows), nc * rows).transpose(1, 2, 0, 3)
    grad_hidden = back.reshape(own, width // nv).astype(bf16)

    dense = dot(hidden_part, gap_rows, ((0,), (0,))).astype(bf16)
    dense = exchange(dense.reshape(cols, rows, block), COLS)
    dense = dense.swapaxes(0, 1).reshape(rows, vocab)
    vocab_ids = lax.axis_index("vocab") * vocab + jnp.arange(vocab, dtype=jnp.int32)
    lookup = (ids[:, None] == vocab_ids[None, :]).astype(bf16)
    head_grad = dot(embed_cols, lookup, ((0,), (0,))) + dense.astype(f32)
    return grad_hidden, head_grad


def solution(mesh):
    torus = Mesh(
        mesh.devices.reshape(2, 4, 4, 2, mesh.shape["vocab"]), ("z", "x", "y", "c", "vocab")
    )
    in_specs = (P(DP, None), P(DP, None), P(DP), P(DP), P(DP, "vocab"), P(DP, "vocab"))
    out_specs = (P(DP, "vocab"), P(DP, "vocab"))
    return jax.shard_map(
        per_device, mesh=torus, in_specs=in_specs, out_specs=out_specs, check_vma=False
    )
```

time: 425 us -> 174 us (0.41)
  waiting for transfers between devices: 294 us -> 84 us
  blocking collectives: 49.2 us -> 17.8 us
  starting transfers between devices: 25.9 us -> 44.2 us
  between operations: 14.6 us -> 0.9 us
  matrix products: 18.1 us -> 9.75 us
  local copies, waits for them, and re-layouts: 14.8 us -> 8.6 us
    reduce_scatter x2 -> x0, waiting for transfers between devices: 210 us -> none  [the longest x1 180 us: sum_by_chip(): return lax.psum_scatter(parts, chips, scatter_dimension=0, tiled=True)[0]]
    all_gather x1 -> x0, waiting for transfers between devices: 77.7 us -> none  [per_device(): gap_piece = lax.all_gather(gap, DP, axis=0, tiled=True)]
    all_to_all x3 -> x7, waiting for transfers between devices: 6.65 us -> 84 us  [exchange(): return lax.all_to_all(x, axes, 0, 0, tiled=True)]
    unnamed x1 -> x0, blocking collectives: 18.7 us -> none
    all_to_all x3 -> x7, starting transfers between devices: 25.8 us -> 44.2 us  [exchange(): return lax.all_to_all(x, axes, 0, 0, tiled=True)]
    all_to_all x2, blocking collectives: 30.4 us -> 17.8 us  [exchange(): return lax.all_to_all(x, axes, 0, 0, tiled=True)]
    dot_general x4, matrix products: 18.1 us -> 9.75 us  [dot(): lax.dot_general(left, right, (contract, ((), ())), preferred_element_type...]
    transpose x2, local copies, waits for them, and re-layouts: 6.86 us -> 0.2 us  [the longest x1 0.16 us: per_device(): embed_out = embed_out.transpose(2, 1, 3, 0, 4).reshape(devices, own, rows)]
  transfers between devices with their start and end apart: 6 -> 7, of which waited for: 5 -> 7; matrix products, arithmetic and copies ran while one was open for 3% -> 7% of each run, Pallas kernels for 0% -> 0%
where the time goes in v1:
time: 174 us; the launch traced here: 172 us
  waiting for transfers between devices  84 us (48%)
  starting transfers between devices  44.2 us (25%)
  blocking collectives  17.8 us (10%)
  matrix products  9.75 us (6%)
  local copies, waits for them, and re-layouts  8.6 us (5%)
  other arithmetic  6.64 us (4%)
    all_to_all x7, waiting for transfers between devices, exchange(): return lax.all_to_all(x, axes, 0, 0, tiled=True)  84 us
    all_to_all x7, starting transfers between devices, exchange(): return lax.all_to_all(x, axes, 0, 0, tiled=True)  44.2 us
    all_to_all x2, blocking collectives, exchange(): return lax.all_to_all(x, axes, 0, 0, tiled=True)  17.8 us
    dot_general x4, matrix products, dot(): lax.dot_general(left, right, (contract, ((), ())), preferred_element_type...  9.75 us
  transfers between devices with their start and end apart: 7, of which 7 were waited for; matrix products, arithmetic and copies ran while one was open for 7% of the time, Pallas kernels for 0%

profile of v1, /device:TPU:2, one launch (start us, length us, event | category | flops | bytes accessed | tf_op | source)
XLA Modules:
  0.0 171.9 jit_solution(12693301099046076261)
XLA Ops:
  0.6 1.4 pad_maximum_fusion
  3.1 6.3 %all-to-all-start.1 = ((bf16[16,72,512]{2,1,0:T(8,128)(2,1)}), bf16[16,72,512]{2,1,0:T(8,128)(2,1)S(1)}, u32[]{:S(2)}, u32[]{:S(2)}) async-start(bf16[16,72,512]{2,1,0:T(8,128)(2,1)} %bitcast.79), calls=%async_computation.1 | async-start | bytes 2359296 | tf_op jit(solution)/shard_map/all_to_all | solution.py:12
  10.2 1.9 %concatenate.10 = bf16[64,8,1152]{2,1,0:T(8,128)(2,1)} concatenate(bf16[64,8,1024]{2,1,0:T(8,128)(2,1)S(1)} %bitcast.90, bf16[64,8,64]{2,1,0:T(8,128)(2,1)S(1)} %bitcast.97, bf16[64,8,64]{2,1,0:T(8,128)(2,1)S(1)} %broadcast_in_dim.12), dimensions={2} | concatenate | bytes 2359296 | tf_op jit(solution)/shard_map/concatenate | solution.py:56
  12.2 12.1 %all-to-all-done.1 = bf16[16,72,512]{2,1,0:T(8,128)(2,1)S(1)} async-done(((bf16[16,72,512]{2,1,0:T(8,128)(2,1)}), bf16[16,72,512]{2,1,0:T(8,128)(2,1)S(1)}, u32[]{:S(2)}, u32[]{:S(2)}) %all-to-all-start.1) | async-done | bytes 1179680 | tf_op jit(solution)/shard_map/all_to_all | solution.py:12
  24.3 9.2 %all-to-all-start = ((bf16[64,8,1152]{2,1,0:T(8,128)(2,1)}), bf16[64,8,1152]{2,1,0:T(8,128)(2,1)S(1)}, u32[]{:S(2)}, u32[]{:S(2)}) async-start(bf16[64,8,1152]{2,1,0:T(8,128)(2,1)} %concatenate.10), calls=%async_computation | async-start | bytes 2359296 | tf_op jit(solution)/shard_map/all_to_all | solution.py:12
  34.6 17.3 %all-to-all-done = bf16[64,8,1152]{2,1,0:T(8,128)(2,1)S(1)} async-done(((bf16[64,8,1152]{2,1,0:T(8,128)(2,1)}), bf16[64,8,1152]{2,1,0:T(8,128)(2,1)S(1)}, u32[]{:S(2)}, u32[]{:S(2)}) %all-to-all-start) | async-done | bytes 1179680 | tf_op jit(solution)/shard_map/all_to_all | solution.py:12
  53.2 1.7 fusion.24
  54.9 4.3 %all-to-all-start.2 = ((f32[4,128,512]{2,1,0:T(8,128)}), f32[4,128,512]{2,1,0:T(8,128)}, u32[]{:S(2)}, u32[]{:S(2)}) async-start(f32[4,128,512]{2,1,0:T(8,128)} %fusion.24), calls=%async_computation.2 | async-start | bytes 2097152 | tf_op jit(solution)/shard_map/all_to_all | solution.py:12
  59.7 13.9 %all-to-all-done.2 = f32[4,128,512]{2,1,0:T(8,128)} async-done(((f32[4,128,512]{2,1,0:T(8,128)}), f32[4,128,512]{2,1,0:T(8,128)}, u32[]{:S(2)}, u32[]{:S(2)}) %all-to-all-start.2) | async-done | bytes 1048608 | tf_op jit(solution)/shard_map/all_to_all | solution.py:12
  73.6 1.3 reduce_sum.63
  75.9 10.7 %all-to-all-start.3 = ((f32[64,4,128]{2,1,0:T(4,128)}), f32[64,4,128]{2,1,0:T(4,128)S(1)}, u32[]{:S(2)}, u32[]{:S(2)}) async-start(f32[64,4,128]{2,1,0:T(4,128)} %broadcast_in_dim.13), calls=%async_computation.3 | async-start | bytes 262144 | tf_op jit(solution)/shard_map/all_to_all | solution.py:12
  87.0 9.0 %all-to-all-done.3 = f32[64,4,128]{2,1,0:T(4,128)S(1)} async-done(((f32[64,4,128]{2,1,0:T(4,128)}), f32[64,4,128]{2,1,0:T(4,128)S(1)}, u32[]{:S(2)}, u32[]{:S(2)}) %all-to-all-start.3) | async-done | bytes 131104 | tf_op jit(solution)/shard_map/all_to_all | solution.py:12
  96.4 12.3 %all_to_all.45 = bf16[4,128,512]{2,1,0:T(8,128)(2,1)S(1)} all-to-all(bf16[4,128,512]{2,1,0:T(8,128)(2,1)S(1)} %broadcast_in_dim.14), channel_id=1, replica_groups=mesh['z'=2,'x'=4,'y'=4,'c'=2,'vocab'=4] {'y'}, dimensions={0} | all-to-all | bytes 1048576 | tf_op jit(solution)/shard_map/all_to_all | solution.py:12
  109.5 2.0 %fusion.25 = f32[2,256,1024]{2,1,0:T(8,128)S(1)} fusion(bf16[2,256,512]{2,1,0:T(8,128)(2,1)S(1)} %bitcast.91, bf16[1024,512,1]{1,0,2:T(8,128)(2,1)} %bitcast.87), kind=kOutput, calls=%fused_computation.58 | convolution fusion | flops 536870912 | bytes 3670016 | tf_op jit(solution)/shard_map/dot_general | solution.py:25
  111.5 5.4 %all_to_all.46 = f32[2,256,1024]{2,1,0:T(8,128)S(1)} all-to-all(f32[2,256,1024]{2,1,0:T(8,128)S(1)} %fusion.25), channel_id=1, replica_groups=mesh['z'=2,'x'=4,'y'=4,'c'=2,'vocab'=4] {'c'}, dimensions={0} | all-to-all | bytes 4194304 | tf_op jit(solution)/shard_map/all_to_all | solution.py:12
  116.9 1.2 reduce_sum.67
  118.1 5.4 %all-to-all-start.6 = ((f32[8,32,1024]{2,1,0:T(8,128)}), f32[8,32,1024]{2,1,0:T(8,128)S(1)}, u32[]{:S(2)}, u32[]{:S(2)}) async-start(f32[8,32,1024]{2,1,0:T(8,128)} %bitcast.89), calls=%async_computation.6 | async-start | bytes 2097152 | tf_op jit(solution)/shard_map/all_to_all | solution.py:12
  123.5 1.7 %convolution_convert_fusion = bf16[1024,512]{1,0:T(8,128)(2,1)} fusion(bf16[512,512]{1,0:T(8,128)(2,1)S(1)} %bitcast.94, bf16[512,1152]{1,0:T(8,128)(2,1)S(1)} %bitcast.83), kind=kOutput, calls=%fused_computation.6 | convolution fusion | flops 537395200 | bytes 2621440 | tf_op jit(solution)/shard_map/dot_general | solution.py:25
  125.3 12.5 %all-to-all-done.6 = f32[8,32,1024]{2,1,0:T(8,128)S(1)} async-done(((f32[8,32,1024]{2,1,0:T(8,128)}), f32[8,32,1024]{2,1,0:T(8,128)S(1)}, u32[]{:S(2)}, u32[]{:S(2)}) %all-to-all-start.6) | async-done | bytes 1048608 | tf_op jit(solution)/shard_map/all_to_all | solution.py:12
  137.8 4.8 %all-to-all-start.8 = ((bf16[16,64,512]{2,1,0:T(8,128)(2,1)}), bf16[16,64,512]{2,1,0:T(8,128)(2,1)S(1)}, u32[]{:S(2)}, u32[]{:S(2)}) async-start(bf16[16,64,512]{2,1,0:T(8,128)(2,1)} %bitcast.95), calls=%async_computation.8 | async-start | bytes 2097152 | tf_op jit(solution)/shard_map/all_to_all | solution.py:12
  143.6 12.3 %all-to-all-done.8 = bf16[16,64,512]{2,1,0:T(8,128)(2,1)S(1)} async-done(((bf16[16,64,512]{2,1,0:T(8,128)(2,1)}), bf16[16,64,512]{2,1,0:T(8,128)(2,1)S(1)}, u32[]{:S(2)}, u32[]{:S(2)}) %all-to-all-start.8) | async-done | bytes 1048608 | tf_op jit(solution)/shard_map/all_to_all | solution.py:12
  156.0 3.5 %all-to-all-start.7 = ((f32[16,8,256]{2,1,0:T(8,128)}), f32[16,8,256]{2,1,0:T(8,128)S(1)}, u32[]{:S(2)}, u32[]{:S(2)}) async-start(f32[16,8,256]{2,1,0:T(8,128)} %bitcast.27), calls=%async_computation.7 | async-start | bytes 262144 | tf_op jit(solution)/shard_map/all_to_all | solution.py:12
  160.0 4.4 %fusion.2 = f32[64,8192]{1,0:T(8,128)} fusion(f32[64,8192]{1,0:T(8,128)S(1)} %bitcast.92, s32[8192]{0:T(1024)S(1)} %iota_add_fusion, s32[512]{0:T(512)S(1)} %fusion.14, bf16[512,1152]{1,0:T(8,128)(2,1)S(1)} %bitcast.85), kind=kOutput, calls=%fused_computation.2 | convolution fusion | flops 541589504 | bytes 4360192 | tf_op jit(solution)/shard_map/dot_general | solution.py:25
  164.4 6.9 %all-to-all-done.7 = f32[16,8,256]{2,1,0:T(8,128)S(1)} async-done(((f32[16,8,256]{2,1,0:T(8,128)}), f32[16,8,256]{2,1,0:T(8,128)S(1)}, u32[]{:S(2)}, u32[]{:S(2)}) %all-to-all-start.7) | async-done | bytes 131104 | tf_op jit(solution)/shard_map/all_to_all | solution.py:12
  (56 shorter events, 9.4 us)
Async XLA Ops:
  2.0 7.4 %copy-start.4 = (bf16[8,4096]{1,0:T(8,128)(2,1)S(1)}, bf16[8,4096]{1,0:T(8,128)(2,1)}, u32[]{:S(2)}) copy-start(bf16[8,4096]{1,0:T(8,128)(2,1)} %param.6) | copy-start | bytes 196612
  2.0 7.5 %copy-start.3 = (bf16[8,4096]{1,0:T(8,128)(2,1)S(1)}, bf16[8,4096]{1,0:T(8,128)(2,1)}, u32[]{:S(2)}) copy-start(bf16[8,4096]{1,0:T(8,128)(2,1)} %param.7) | copy-start | bytes 196612
  3.1 6.8 %copy-start.6 = (s32[8]{0:T(128)S(1)}, s32[8]{0:T(128)}, u32[]{:S(2)}) copy-start(s32[8]{0:T(128)} %param.8) | copy-start | bytes 100
  3.1 6.8 %copy-start.5 = (f32[8]{0:T(128)S(1)}, f32[8]{0:T(128)}, u32[]{:S(2)}) copy-start(f32[8]{0:T(128)} %param.9) | copy-start | bytes 100
  3.1 21.2 %all-to-all-start.1 = ((bf16[16,72,512]{2,1,0:T(8,128)(2,1)}), bf16[16,72,512]{2,1,0:T(8,128)(2,1)S(1)}, u32[]{:S(2)}, u32[]{:S(2)}) async-start(bf16[16,72,512]{2,1,0:T(8,128)(2,1)} %bitcast.79), calls=%async_computation.1 | async-start | bytes 2359296 | tf_op jit(solution)/shard_map/all_to_all | solution.py:12
  24.3 27.7 %all-to-all-start = ((bf16[64,8,1152]{2,1,0:T(8,128)(2,1)}), bf16[64,8,1152]{2,1,0:T(8,128)(2,1)S(1)}, u32[]{:S(2)}, u32[]{:S(2)}) async-start(bf16[64,8,1152]{2,1,0:T(8,128)(2,1)} %concatenate.10), calls=%async_computation | async-start | bytes 2359296 | tf_op jit(solution)/shard_map/all_to_all | solution.py:12
  52.0 1.2 copy-start
  54.9 18.7 %all-to-all-start.2 = ((f32[4,128,512]{2,1,0:T(8,128)}), f32[4,128,512]{2,1,0:T(8,128)}, u32[]{:S(2)}, u32[]{:S(2)}) async-start(f32[4,128,512]{2,1,0:T(8,128)} %fusion.24), calls=%async_computation.2 | async-start | bytes 2097152 | tf_op jit(solution)/shard_map/all_to_all | solution.py:12
  75.9 20.1 %all-to-all-start.3 = ((f32[64,4,128]{2,1,0:T(4,128)}), f32[64,4,128]{2,1,0:T(4,128)S(1)}, u32[]{:S(2)}, u32[]{:S(2)}) async-start(f32[64,4,128]{2,1,0:T(4,128)} %broadcast_in_dim.13), calls=%async_computation.3 | async-start | bytes 262144 | tf_op jit(solution)/shard_map/all_to_all | solution.py:12
  108.7 0.8 copy-start.1
  118.1 5.4 %copy-start.2 = (bf16[4,128,512]{2,1,0:T(8,128)(2,1)S(1)}, bf16[4,128,512]{2,1,0:T(8,128)(2,1)}, u32[]{:S(2)}) copy-start(bf16[4,128,512]{2,1,0:T(8,128)(2,1)} %copy-done.1) | copy-start | bytes 1572868
  118.1 19.6 %all-to-all-start.6 = ((f32[8,32,1024]{2,1,0:T(8,128)}), f32[8,32,1024]{2,1,0:T(8,128)S(1)}, u32[]{:S(2)}, u32[]{:S(2)}) async-start(f32[8,32,1024]{2,1,0:T(8,128)} %bitcast.89), calls=%async_computation.6 | async-start | bytes 2097152 | tf_op jit(solution)/shard_map/all_to_all | solution.py:12
  137.8 18.2 %all-to-all-start.8 = ((bf16[16,64,512]{2,1,0:T(8,128)(2,1)}), bf16[16,64,512]{2,1,0:T(8,128)(2,1)S(1)}, u32[]{:S(2)}, u32[]{:S(2)}) async-start(bf16[16,64,512]{2,1,0:T(8,128)(2,1)} %bitcast.95), calls=%async_computation.8 | async-start | bytes 2097152 | tf_op jit(solution)/shard_map/all_to_all | solution.py:12
  156.0 15.3 %all-to-all-start.7 = ((f32[16,8,256]{2,1,0:T(8,128)}), f32[16,8,256]{2,1,0:T(8,128)S(1)}, u32[]{:S(2)}, u32[]{:S(2)}) async-start(f32[16,8,256]{2,1,0:T(8,128)} %bitcast.27), calls=%async_computation.7 | async-start | bytes 262144 | tf_op jit(solution)/shard_map/all_to_all | solution.py:12
